TPU v7x, 32 devices: a whole 2x2x4 slice. The times are simulated.
32 devices in a mesh: scan: 16 (over z, x, core), tile: 2 (over y).
Axes of the slice: x: 2, y: 2, z: 4, core: 2. Of those that a mesh axis runs over, the one named last changes fastest.
Arguments:
- probe_modes: float32 [12, 2, 128, 128], replicated, may hold values from -5 to 5
- patterns: float32 [128, 128, 128], P(('scan', 'tile')), may hold values from 0.005 to 300
- specimen: float32 [2, 2048, 512], P(None, 'scan', 'tile'), may hold values from -17.5 to 17.5
- offsets: int32 [128, 2], P(('scan', 'tile')), may hold values from -128 to 2048, as said below
Outputs:
- new_probe: float32 [12, 2, 128, 128], replicated
- new_specimen: float32 [2, 2048, 512], P(None, 'scan', 'tile')
Inputs may be any that keep to these rules, and one draw needn't show every extreme that they name: `offsets`: position p lies in aligned block b = p // 4, held by the device of scan index s = b // (the number of tile devices) and tile index t = b % (the number of tile devices); its row offset lies in s * 128 - 128 to s * 128 + 128, its column offset in t * 256 - 128 to t * 256 + 256, both ends included; in every block one position has its row offset at the lower end and its column offset at the upper end, and one has its row offset at the upper end.
All inputs are finite; a program needn't handle non-finite values.
Results may differ from a plain program's by a relative error of at most 0.0001.
Values sent between devices are 32-bit elements; how exact they have to be, the bound alone decides.
A program may use at most 64 MiB of HBM per device.

v0:
```python
import math
import jax
import jax.numpy as jnp
from jax import lax
from jax.sharding import PartitionSpec as P

NS_STEPS = 8
highest = lax.Precision.HIGHEST
light_floor = 0.05
object_reg = 0.5
probe_reg = 1.0
total_eps = 1e-06


def extended_2(array, sides, width):
    for axis, dim in sides:
        size, length = (lax.axis_size(axis), array.shape[dim])
        up = [(i, (i + 1) % size) for i in range(size - 1)]
        down = [(j, i) for i, j in up]
        last = lax.slice_in_dim(array, length - width, length, axis=dim)
        first = lax.slice_in_dim(array, 0, width, axis=dim)
        before = lax.ppermute(last, axis, up)
        after = lax.ppermute(first, axis, down)
        array = jnp.concatenate([before, array, after], axis=dim)
    return array


def dft_tables(detector):
    indices = jnp.arange(detector, dtype=jnp.int32)
    product = indices[:, None] * indices[None, :] % detector
    angles = -2.0 * math.pi / detector * product.astype(jnp.float32)
    norm_factor = 1.0 / math.sqrt(detector)
    return (jnp.cos(angles) * norm_factor, jnp.sin(angles) * norm_factor)


def complex_section(real_part, imag_part, table, direction, on_right):
    stacked = jnp.stack([real_part, imag_part])
    if on_right:
        products = jnp.einsum(
            "cmxy,yw->cmxw", stacked, table, precision=highest, preferred_element_type=jnp.float32
        )
        split_at = real_part.shape[-1]
        plain_re, twist_re = (products[0, :, :, :split_at], products[0, :, :, split_at:])
        plain_im, twist_im = (products[1, :, :, :split_at], products[1, :, :, split_at:])
    else:
        products = jnp.einsum(
            "wx,cmxy->cmwy", table, stacked, precision=highest, preferred_element_type=jnp.float32
        )
        split_at = real_part.shape[-2]
        plain_re, twist_re = (products[0, :, :split_at], products[0, :, split_at:])
        plain_im, twist_im = (products[1, :, :split_at], products[1, :, split_at:])
    return (plain_re - direction * twist_im, direction * twist_re + plain_im)


def newton_steps(gram_re, gram_im):
    mode_count = gram_re.shape[0]
    upper = jnp.concatenate([gram_re, -gram_im], axis=1)
    lower = jnp.concatenate([gram_im, gram_re], axis=1)
    embedded = jnp.concatenate([upper, lower], axis=0)
    frobenius = jnp.sqrt(jnp.sum(embedded * embedded))
    identity = jnp.eye(2 * mode_count, dtype=jnp.float32)
    current = embedded / frobenius
    inverse = identity
    for repeat in range(NS_STEPS):
        factor = 1.5 * identity - 0.5 * jnp.dot(
            inverse, current, precision=highest, preferred_element_type=jnp.float32
        )
        current = jnp.dot(current, factor, precision=highest, preferred_element_type=jnp.float32)
        inverse = jnp.dot(factor, inverse, precision=highest, preferred_element_type=jnp.float32)
    inverse = inverse / jnp.sqrt(frobenius)
    return (inverse[:mode_count, :mode_count], inverse[mode_count:, :mode_count])


def gram_parts(mode_rows):
    real_rows = mode_rows[0::2]
    imag_rows = mode_rows[1::2]
    gram_re = jnp.dot(
        real_rows, real_rows.T, precision=highest, preferred_element_type=jnp.float32
    ) + jnp.dot(imag_rows, imag_rows.T, precision=highest, preferred_element_type=jnp.float32)
    gram_im = jnp.dot(
        real_rows, imag_rows.T, precision=highest, preferred_element_type=jnp.float32
    ) - jnp.dot(imag_rows, real_rows.T, precision=highest, preferred_element_type=jnp.float32)
    return (gram_re, gram_im)


def orthonormal_rows(mode_rows, gram_re, gram_im, power_ratio):
    real_rows = mode_rows[0::2]
    imag_rows = mode_rows[1::2]
    mix_re, mix_im = newton_steps(gram_re, gram_im)
    ortho_re = jnp.dot(
        mix_re.T, real_rows, precision=highest, preferred_element_type=jnp.float32
    ) - jnp.dot(mix_im.T, imag_rows, precision=highest, preferred_element_type=jnp.float32)
    ortho_im = jnp.dot(
        mix_im.T, real_rows, precision=highest, preferred_element_type=jnp.float32
    ) + jnp.dot(mix_re.T, imag_rows, precision=highest, preferred_element_type=jnp.float32)
    weight = jnp.sqrt(power_ratio * jnp.diagonal(gram_re))
    joined = jnp.stack([ortho_re, ortho_im], axis=1) * weight[:, None, None]
    return joined.reshape(mode_rows.shape)


def global_totals(measured, modeled):
    return lax.psum((measured, modeled), ("scan", "tile"))


def fold_interior(frame_sum, folded, detector, block_rows, block_cols):
    rows_end = block_rows + 3 * detector
    cols_end = block_cols + 3 * detector
    centre_rows = slice(2 * detector, 2 * detector + block_rows)
    centre_cols = slice(2 * detector, 2 * detector + block_cols)
    interior = frame_sum[:, detector : detector + block_rows, detector : detector + block_cols]
    interior = interior.at[:, :detector, :].add(folded[:, :detector, centre_cols])
    interior = interior.at[:, block_rows - detector :, :].add(folded[:, rows_end:, centre_cols])
    interior = interior.at[:, :, :detector].add(folded[:, centre_rows, :detector])
    interior = interior.at[:, :, block_cols - detector :].add(folded[:, centre_rows, cols_end:])
    interior = interior.at[:, :detector, :detector].add(folded[:, :detector, :detector])
    interior = interior.at[:, :detector, block_cols - detector :].add(
        folded[:, :detector, cols_end:]
    )
    interior = interior.at[:, block_rows - detector :, :detector].add(
        folded[:, rows_end:, :detector]
    )
    interior = interior.at[:, block_rows - detector :, block_cols - detector :].add(
        folded[:, rows_end:, cols_end:]
    )
    return interior


def body(probe_modes, patterns, specimen, offsets):
    detector = probe_modes.shape[-1]
    mode_count = probe_modes.shape[0]
    block_rows = specimen.shape[1]
    block_cols = specimen.shape[2]
    position_count = patterns.shape[0]
    table_re, table_im = dft_tables(detector)
    right_table = jnp.concatenate([table_re, table_im], axis=1)
    left_table = jnp.concatenate([table_re, table_im], axis=0)
    probe_re = probe_modes[:, 0]
    probe_im = probe_modes[:, 1]
    probe_power = jnp.sum(probe_re * probe_re + probe_im * probe_im, axis=0)
    extended = extended_2(specimen, (("scan", 1), ("tile", 2)), detector)
    row_base = lax.axis_index("scan") * block_rows - detector
    col_base = lax.axis_index("tile") * block_cols - detector
    local_rows = offsets[:, 0] - row_base
    local_cols = offsets[:, 1] - col_base
    zero_index = jnp.zeros((), jnp.int32)
    channels = 3

    def patch_at(position):
        return lax.dynamic_slice(
            extended,
            (zero_index, local_rows[position], local_cols[position]),
            (2, detector, detector),
        )

    def one_position(position, running):
        grad_re, grad_im, light_sum, frame_sum, model_sum = running
        patch_now = patch_at(position)
        patch_re = patch_now[0]
        patch_im = patch_now[1]
        exit_re = probe_re * patch_re[None] - probe_im * patch_im[None]
        exit_im = probe_re * patch_im[None] + probe_im * patch_re[None]
        model_sum = model_sum + jnp.sum(exit_re * exit_re + exit_im * exit_im)
        half_re, half_im = complex_section(exit_re, exit_im, right_table, 1.0, True)
        far_re, far_im = complex_section(half_re, half_im, left_table, 1.0, False)
        model_light = jnp.sum(far_re * far_re + far_im * far_im, axis=0)
        factor = (
            jnp.sqrt(patterns[position]) / jnp.sqrt(jnp.maximum(model_light, light_floor)) - 1.0
        )
        back_re, back_im = complex_section(
            far_re * factor[None], far_im * factor[None], right_table, -1.0, True
        )
        change_re, change_im = complex_section(back_re, back_im, left_table, -1.0, False)
        grad_re = grad_re + patch_re[None] * change_re + patch_im[None] * change_im
        grad_im = grad_im + patch_re[None] * change_im - patch_im[None] * change_re
        light_sum = light_sum + patch_re * patch_re + patch_im * patch_im
        num_re = jnp.sum(probe_re * change_re + probe_im * change_im, axis=0)
        num_im = jnp.sum(probe_re * change_im - probe_im * change_re, axis=0)
        addition = jnp.stack([num_re, num_im, probe_power])
        row_at = local_rows[position]
        col_at = local_cols[position]
        previous = lax.dynamic_slice(
            frame_sum, (zero_index, row_at, col_at), (channels, detector, detector)
        )
        frame_sum = lax.dynamic_update_slice(
            frame_sum, previous + addition, (zero_index, row_at, col_at)
        )
        return (grad_re, grad_im, light_sum, frame_sum, model_sum)

    mode_zeros = jnp.zeros((mode_count, detector, detector), jnp.float32)
    frame_init = jnp.zeros(
        (channels, block_rows + 2 * detector, block_cols + 2 * detector), jnp.float32
    )
    initial = (
        mode_zeros,
        mode_zeros,
        jnp.zeros((detector, detector), jnp.float32),
        frame_init,
        jnp.zeros((), jnp.float32),
    )
    grad_re, grad_im, light_sum, frame_sum, model_sum = lax.fori_loop(
        0, position_count, one_position, initial
    )
    measured_all, model_all = global_totals(jnp.sum(patterns), model_sum)
    power_ratio = measured_all / (model_all + total_eps)
    folded = extended_2(frame_sum, (("scan", 1), ("tile", 2)), detector)
    interior = fold_interior(frame_sum, folded, detector, block_rows, block_cols)
    interior_num = interior[0:2]
    interior_light = interior[2]
    new_specimen = specimen + interior_num / (interior_light + object_reg)[None]
    grad_rows = jnp.stack([grad_re, grad_im], axis=1).reshape(2 * mode_count, -1)
    light_row = light_sum.reshape(1, -1)
    probe_rows = probe_modes.reshape(2 * mode_count, -1)
    grad_total, light_total = lax.psum((grad_rows, light_row), ("scan", "tile"))
    updated = probe_rows + grad_total / (light_total + probe_reg)
    gram_re, gram_im = gram_parts(updated)
    new_probe = orthonormal_rows(updated, gram_re, gram_im, power_ratio).reshape(probe_modes.shape)
    return (new_probe, new_specimen)


def solution(mesh):
    return jax.shard_map(
        body,
        mesh=mesh,
        in_specs=(
            P(),
            P(("scan", "tile"), None, None),
            P(None, "scan", "tile"),
            P(("scan", "tile"), None),
        ),
        out_specs=(P(), P(None, "scan", "tile")),
        check_vma=False,
    )
```

profile of v0, /device:TPU:0, one launch (start us, length us, event | category | flops | bytes accessed | tf_op | source)
XLA Modules:
  0.0 347.7 jit_solution(15075586222732396307)
XLA Ops:
  8.7 3.1 collective-permute-start
  15.1 5.1 %collective-permute-start.2 = (f32[2,384,128]{2,1,0:T(8,128)S(1)}, f32[2,384,128]{2,1,0:T(8,128)S(1)}, u32[]{:S(2)}, u32[]{:S(2)}) collective-permute-start(f32[2,384,128]{2,1,0:T(8,128)S(1)} %get-tuple-element.611), channel_id=1, source_target_pairs={{0,1},{2,3},{4,5},{6,7},{8,9},{10,11},{12,13},{14,15},{16,17},{18,... | collective-permute-start | bytes 1179656 | tf_op jit(solution)/shard_map/ppermute | solution.py:22
  21.6 5.7 %collective-permute-done.2 = f32[2,384,128]{2,1,0:T(8,128)S(1)} collective-permute-done((f32[2,384,128]{2,1,0:T(8,128)S(1)}, f32[2,384,128]{2,1,0:T(8,128)S(1)}, u32[]{:S(2)}, u32[]{:S(2)}) %collective-permute-start.2) | collective-permute-done | bytes 393248 | tf_op jit(solution)/shard_map/ppermute | solution.py:22
  27.4 4.7 %collective-permute-done.3 = f32[2,384,128]{2,1,0:T(8,128)S(1)} collective-permute-done((f32[2,384,128]{2,1,0:T(8,128)S(1)}, f32[2,384,128]{2,1,0:T(8,128)S(1)}, u32[]{:S(2)}, u32[]{:S(2)}) %collective-permute-start.3) | collective-permute-done | bytes 393248 | tf_op jit(solution)/shard_map/ppermute | solution.py:23
  35.1 113.1 %while.34 = (s32[]{:T(128)}, f32[12,128,128]{2,1,0:T(8,128)}, f32[12,128,128]{2,1,0:T(8,128)}, f32[128,128]{1,0:T(8,128)}, f32[3,384,512]{2,1,0:T(8,128)}, /*ind...) while((s32[]{:T(128)}, f32[12,128,128]{2,1,0:T(8,128)}, ...), condition=%wide.region_6.7_spmd.clone, body=%wide.region_1.6_spmd.clone.sunk | while | flops 4844257280 | bytes 53870996 | solution.py:200
  45.4 2.8 convolution_bitcast_fusion.4
  48.6 2.8 fusion.164
  51.6 2.7 convolution_bitcast_fusion.5
  58.8 2.8 dynamic_update_slice.12
  72.0 2.8 convolution_bitcast_fusion.4
  75.2 2.8 fusion.164
  78.2 2.7 convolution_bitcast_fusion.5
  82.9 2.8 fusion.166
  86.9 2.8 dynamic_update_slice.12
  100.1 2.8 convolution_bitcast_fusion.4
  103.3 2.8 fusion.164
  106.3 2.7 convolution_bitcast_fusion.5
  111.0 2.8 fusion.166
  115.0 4.0 %dynamic_update_slice.12 = f32[3,384,512]{2,1,0:T(8,128)} dynamic-update-slice(f32[3,384,512]{2,1,0:T(8,128)} %get-tuple-element.770, f32[3,128,128]{2,1,0:T(8,128)S(1)} %maximum_add_fusion.2, s32[]{:T(128)} %constant.327.clone.1..sunk, s32[]{:T(128)S(6)} %select_n.67, s32[]{:T(128)S(6)} %select_n.68) | dynamic-update-slice | bytes 393220 | tf_op jit(solution)/shard_map/while/body/eval_jaxpr/dynamic_update_slice | solution.py:184
  129.4 2.8 convolution_bitcast_fusion.4
  132.6 2.8 fusion.164
  135.6 2.7 convolution_bitcast_fusion.5
  140.3 2.8 fusion.166
  144.3 4.0 %dynamic_update_slice.12 = f32[3,384,512]{2,1,0:T(8,128)} dynamic-update-slice(f32[3,384,512]{2,1,0:T(8,128)} %get-tuple-element.770, f32[3,128,128]{2,1,0:T(8,128)S(1)} %maximum_add_fusion.2, s32[]{:T(128)} %constant.327.clone.1..sunk, s32[]{:T(128)S(6)} %select_n.67, s32[]{:T(128)S(6)} %select_n.68) | dynamic-update-slice | bytes 393220 | tf_op jit(solution)/shard_map/while/body/eval_jaxpr/dynamic_update_slice | solution.py:184
  148.3 2.8 fusion.66
  151.1 3.7 %collective-permute-start.4 = (f32[3,128,512]{2,1,0:T(8,128)}, f32[3,128,512]{2,1,0:T(8,128)S(1)}, u32[]{:S(2)}, u32[]{:S(2)}) collective-permute-start(f32[3,128,512]{2,1,0:T(8,128)} %get-tuple-element.607), channel_id=1, source_target_pairs={{0,2},{2,4},{4,6},{6,8},{8,10},{10,12},{12,14},{14,16},{16,18},{18... | collective-permute-start | bytes 2359304 | tf_op jit(solution)/shard_map/ppermute | solution.py:22
  160.1 51.6 %all-reduce = (f32[]{:T(128)}, f32[]{:T(128)}) all-reduce(f32[]{:T(128)} %reduce_sum.93, f32[]{:T(128)} %get-tuple-element.473), channel_id=1, replica_groups=mesh['scan'=16,'tile'=2] {'scan','tile'}, use_global_device_ids=true, to_apply=%region_11.12 | all-reduce | flops 2 | bytes 16 | tf_op jit(solution)/shard_map/psum | solution.py:102
  219.0 6.4 %collective-permute-start.6 = (f32[3,640,128]{2,1,0:T(8,128)}, f32[3,640,128]{2,1,0:T(8,128)}, u32[]{:S(2)}, u32[]{:S(2)}) collective-permute-start(f32[3,640,128]{2,1,0:T(8,128)} %get-tuple-element.606), channel_id=1, source_target_pairs={{0,1},{2,3},{4,5},{6,7},{8,9},{10,11},{12,13},{14,15},{16,17},{18,... | collective-permute-start | bytes 2949128 | tf_op jit(solution)/shard_map/ppermute | solution.py:22
  226.7 70.5 %all-reduce.4.cloned.1.call-done = (f32[24,16384]{1,0:T(8,128)}, f32[1,16384]{1,0:T(1,128)}) async-done(((f32[24,16384]{1,0:T(8,128)}, f32[1,16384]{1,0:T(1,128)}), (f32[24,16384]{1,0:T(8,128)}, f32[1,16384]{1,0:T(1,128)})) %all-reduce.4.cloned.1.call-update) | async-done | bytes 1638416 | tf_op jit(solution)/shard_map/psum | solution.py:213
  298.1 3.5 %bitcast_add_fusion = f32[24,16384]{1,0:T(8,128)} fusion(f32[3,8,128,128]{3,2,1,0:T(8,128)S(1)} %bitcast.192, f32[24,16384]{1,0:T(8,128)} %get-tuple-element.588, f32[16384]{0:T(1024)S(1)} %bitcast.201), kind=kLoop, calls=%fused_computation.67 | loop fusion | flops 786432 | bytes 4784128 | tf_op jit(solution)/shard_map/add | solution.py:214
  301.6 5.7 %slice.446 = f32[12,16384]{1,0:T(8,128)S(1)} slice(f32[24,16384]{1,0:T(8,128)} %bitcast_add_fusion), slice={[1:24:2], [0:16384:1]} | slice | bytes 1572864 | tf_op jit(solution)/shard_map/slice | solution.py:76
  307.3 5.7 %slice.445 = f32[12,16384]{1,0:T(8,128)S(1)} slice(f32[24,16384]{1,0:T(8,128)} %bitcast_add_fusion), slice={[0:24:2], [0:16384:1]} | slice | bytes 1572864 | tf_op jit(solution)/shard_map/slice | solution.py:75
  (178 shorter events, 91.1 us)
Async XLA Ops:
  7.2 7.8 %copy-start.10 = (f32[2,128,256]{2,1,0:T(8,128)S(1)}, f32[2,128,256]{2,1,0:T(8,128)}, u32[]{:S(2)}) copy-start(f32[2,128,256]{2,1,0:T(8,128)} %param.28) | copy-start | bytes 786436
  7.2 290.0 %all-reduce.4.cloned.1.call-start = ((), (), s32[]{:S(2)}) async-start(), calls=%async_computation | async-start | bytes 3276800 | tf_op jit(solution)/shard_map/psum | solution.py:213
  7.2 7.8 %collective-permute-start.1 = (f32[2,128,256]{2,1,0:T(8,128)}, f32[2,128,256]{2,1,0:T(8,128)S(1)}, u32[]{:S(2)}, u32[]{:S(2)}) collective-permute-start(f32[2,128,256]{2,1,0:T(8,128)} %param.28), channel_id=1, source_target_pairs={{2,0},{4,2},{6,4},{8,6},{10,8},{12,10},{14,12},{16,14},{18,16},{20... | collective-permute-start | bytes 786440 | tf_op jit(solution)/shard_map/ppermute | solution.py:23
  8.7 6.3 %collective-permute-start = (f32[2,128,256]{2,1,0:T(8,128)}, f32[2,128,256]{2,1,0:T(8,128)S(1)}, u32[]{:S(2)}, u32[]{:S(2)}) collective-permute-start(f32[2,128,256]{2,1,0:T(8,128)} %param.28), channel_id=1, source_target_pairs={{0,2},{2,4},{4,6},{6,8},{8,10},{10,12},{12,14},{14,16},{16,18},{18... | collective-permute-start | bytes 786440 | tf_op jit(solution)/shard_map/ppermute | solution.py:22
  15.0 6.5 %copy-start.2 = (f32[12,2,128,128]{3,2,1,0:T(8,128)S(1)}, f32[12,2,128,128]{3,2,1,0:T(8,128)}, u32[]{:S(2)}) copy-start(f32[12,2,128,128]{3,2,1,0:T(8,128)} %param.26) | copy-start | bytes 4718596
  15.1 12.2 %collective-permute-start.2 = (f32[2,384,128]{2,1,0:T(8,128)S(1)}, f32[2,384,128]{2,1,0:T(8,128)S(1)}, u32[]{:S(2)}, u32[]{:S(2)}) collective-permute-start(f32[2,384,128]{2,1,0:T(8,128)S(1)} %get-tuple-element.611), channel_id=1, source_target_pairs={{0,1},{2,3},{4,5},{6,7},{8,9},{10,11},{12,13},{14,15},{16,17},{18,... | collective-permute-start | bytes 1179656 | tf_op jit(solution)/shard_map/ppermute | solution.py:22
  20.2 11.9 %collective-permute-start.3 = (f32[2,384,128]{2,1,0:T(8,128)S(1)}, f32[2,384,128]{2,1,0:T(8,128)S(1)}, u32[]{:S(2)}, u32[]{:S(2)}) collective-permute-start(f32[2,384,128]{2,1,0:T(8,128)S(1)} %get-tuple-element.612), channel_id=1, source_target_pairs={{1,0},{3,2},{5,4},{7,6},{9,8},{11,10},{13,12},{15,14},{17,16},{19,... | collective-permute-start | bytes 1179656 | tf_op jit(solution)/shard_map/ppermute | solution.py:23
  56.2 1.4 copy-start.4
  56.3 1.4 copy-start.5
  82.8 2.8 copy-start.4
  82.9 2.8 copy-start.5
  111.0 2.8 copy-start.4
  111.0 2.8 copy-start.5
  140.2 2.8 copy-start.4
  140.2 2.8 copy-start.5
  148.2 9.6 %copy-start = (f32[12,128,128]{2,1,0:T(8,128)S(1)}, f32[12,128,128]{2,1,0:T(8,128)}, u32[]{:S(2)}) copy-start(f32[12,128,128]{2,1,0:T(8,128)} %get-tuple-element.471) | copy-start | bytes 2359300
  148.2 9.6 %copy-start.1 = (f32[12,128,128]{2,1,0:T(8,128)S(1)}, f32[12,128,128]{2,1,0:T(8,128)}, u32[]{:S(2)}) copy-start(f32[12,128,128]{2,1,0:T(8,128)} %get-tuple-element.470) | copy-start | bytes 2359300
  151.1 61.9 %collective-permute-start.4 = (f32[3,128,512]{2,1,0:T(8,128)}, f32[3,128,512]{2,1,0:T(8,128)S(1)}, u32[]{:S(2)}, u32[]{:S(2)}) collective-permute-start(f32[3,128,512]{2,1,0:T(8,128)} %get-tuple-element.607), channel_id=1, source_target_pairs={{0,2},{2,4},{4,6},{6,8},{8,10},{10,12},{12,14},{14,16},{16,18},{18... | collective-permute-start | bytes 2359304 | tf_op jit(solution)/shard_map/ppermute | solution.py:22
  154.8 60.4 %collective-permute-start.5 = (f32[3,128,512]{2,1,0:T(8,128)}, f32[3,128,512]{2,1,0:T(8,128)S(1)}, u32[]{:S(2)}, u32[]{:S(2)}) collective-permute-start(f32[3,128,512]{2,1,0:T(8,128)} %get-tuple-element.608), channel_id=1, source_target_pairs={{2,0},{4,2},{6,4},{8,6},{10,8},{12,10},{14,12},{16,14},{18,16},{20... | collective-permute-start | bytes 2359304 | tf_op jit(solution)/shard_map/ppermute | solution.py:23
  213.0 2.2 copy-start.7
  215.2 1.0 copy-start.9
  216.2 9.3 %copy-start.8 = (f32[3,128,512]{2,1,0:T(8,128)S(1)}, f32[3,128,512]{2,1,0:T(8,128)}, u32[]{:S(2)}) copy-start(f32[3,128,512]{2,1,0:T(8,128)} %copy-done.7) | copy-start | bytes 2359300
  217.6 80.4 %copy-start.3 = (f32[12,2,128,128]{3,2,1,0:T(8,128)S(1)}, f32[12,2,128,128]{3,2,1,0:T(8,128)}, u32[]{:S(2)}) copy-start(f32[12,2,128,128]{3,2,1,0:T(8,128)} %param.26) | copy-start | bytes 4718596
  217.6 117.6 %collective-permute-start.7 = (f32[3,640,128]{2,1,0:T(8,128)}, f32[3,640,128]{2,1,0:T(8,128)}, u32[]{:S(2)}, u32[]{:S(2)}) collective-permute-start(f32[3,640,128]{2,1,0:T(8,128)} %get-tuple-element.605), channel_id=1, source_target_pairs={{1,0},{3,2},{5,4},{7,6},{9,8},{11,10},{13,12},{15,14},{17,16},{19,... | collective-permute-start | bytes 2949128 | tf_op jit(solution)/shard_map/ppermute | solution.py:23
  219.0 115.2 %collective-permute-start.6 = (f32[3,640,128]{2,1,0:T(8,128)}, f32[3,640,128]{2,1,0:T(8,128)}, u32[]{:S(2)}, u32[]{:S(2)}) collective-permute-start(f32[3,640,128]{2,1,0:T(8,128)} %get-tuple-element.606), channel_id=1, source_target_pairs={{0,1},{2,3},{4,5},{6,7},{8,9},{10,11},{12,13},{14,15},{16,17},{18,... | collective-permute-start | bytes 2949128 | tf_op jit(solution)/shard_map/ppermute | solution.py:22
  328.8 2.4 copy-start.6
  335.2 5.0 %copy-start.11 = (f32[2,128,256]{2,1,0:T(8,128)S(1)}, f32[2,128,256]{2,1,0:T(8,128)}, u32[]{:S(2)}) copy-start(f32[2,128,256]{2,1,0:T(8,128)} %param.28) | copy-start | bytes 786436
Sparse Core Ops, SparseCore 0:
  160.2 136.8 all-reduce.3
where the time goes:
time: 350 us; the launch traced here: 348 us
  waiting for transfers between devices  81 us (23%)
  matrix products  60.7 us (17%)
  blocking collectives  51.6 us (15%)
  other arithmetic  51.5 us (15%)
  local copies, waits for them, and re-layouts  46.2 us (13%)
  starting transfers between devices  23.7 us (7%)
  between operations  16.5 us (5%)
  loops' own time  16.4 us (5%)
    psum x1, waiting for transfers between devices, body(): grad_total, light_total = lax.psum((grad_rows, light_row), ('scan', 'tile'))  70.5 us
    psum x1, blocking collectives, global_totals(): return lax.psum((measured, modeled), ('scan', 'tile'))  51.6 us
    dot_general x8, matrix products, complex_section(): jnp.einsum('wx,cmxy->cmwy', table, stacked, precision=highest, preferred_...  22 us
    dot_general x8, matrix products, complex_section(): jnp.einsum('cmxy,yw->cmxw', stacked, table, precision=highest, preferred_...  21.8 us
    ppermute x4, starting transfers between devices, extended_2(): before = lax.ppermute(last, axis, up)  18.2 us
    another operation x1, loops' own time, body(): lax.fori_loop(0, position_count, one_position, initial)  16.4 us
    dynamic_update_slice x4, local copies, waits for them, and re-layouts, one_position(): lax.dynamic_update_slice(frame_sum, previous + addition, (zero_index, row...  13.6 us
    sub x4, other arithmetic, one_position(): grad_im = grad_im + patch_re[None] * change_im - patch_im[None] * change_re  9.88 us
  transfers between devices with their start and end apart: 9, of which 3 were waited for; matrix products, arithmetic and copies ran while one was open for 14% of the time, Pallas kernels for 0%

commit v1 on v0

--- a/solution.py
+++ b/solution.py
@@ -210,7 +210,9 @@
     grad_rows = jnp.stack([grad_re, grad_im], axis=1).reshape(2 * mode_count, -1)
     light_row = light_sum.reshape(1, -1)
     probe_rows = probe_modes.reshape(2 * mode_count, -1)
-    grad_total, light_total = lax.psum((grad_rows, light_row), ("scan", "tile"))
+    grad_total, light_total = jax.lax.psum(
+        jax.lax.psum((grad_rows, light_row), axis_name="tile"), axis_name="scan"
+    )
     updated = probe_rows + grad_total / (light_total + probe_reg)
     gram_re, gram_im = gram_parts(updated)
     new_probe = orthonormal_rows(updated, gram_re, gram_im, power_ratio).reshape(probe_modes.shape)

time: 350 us -> 389 us (1.11)
  blocking collectives: 51.6 us -> 73.1 us
  waiting for transfers between devices: 81 us -> 101 us
  starting transfers between devices: 23.7 us -> 19.6 us
    psum x1, blocking collectives: 51.6 us -> 73.1 us  [global_totals(): return lax.psum((measured, modeled), ('scan', 'tile'))]
    psum x1 -> x2, waiting for transfers between devices: 70.5 us -> 89.1 us  [the longest x1 89.1 us: body(): jax.lax.psum(jax.lax.psum((grad_rows, light_row), axis_name='tile'), axis...]
    ppermute x4, starting transfers between devices: 18.2 us -> 14.2 us  [extended_2(): before = lax.ppermute(last, axis, up)]
  transfers between devices with their start and end apart: 9 -> 10, of which waited for: 3 -> 4; matrix products, arithmetic and copies ran while one was open for 14% -> 5% of each run, Pallas kernels for 0% -> 0%
where the time goes in v1:
time: 389 us; the launch traced here: 387 us
  waiting for transfers between devices  101 us (26%)
  blocking collectives  73.1 us (19%)
  matrix products  59.7 us (15%)
  other arithmetic  50.5 us (13%)
  local copies, waits for them, and re-layouts  46.8 us (12%)
  starting transfers between devices  19.6 us (5%)
  loops' own time  19.6 us (5%)
  between operations  16.6 us (4%)
    psum x1, waiting for transfers between devices, body(): jax.lax.psum(jax.lax.psum((grad_rows, light_row), axis_name='tile'), axis...  89.1 us
    psum x1, blocking collectives, global_totals(): return lax.psum((measured, modeled), ('scan', 'tile'))  73.1 us
    dot_general x8, matrix products, complex_section(): jnp.einsum('wx,cmxy->cmwy', table, stacked, precision=highest, preferred_...  21.9 us
    dot_general x8, matrix products, complex_section(): jnp.einsum('cmxy,yw->cmxw', stacked, table, precision=highest, preferred_...  21.8 us
    another operation x1, loops' own time, body(): lax.fori_loop(0, position_count, one_position, initial)  19.6 us
    ppermute x4, starting transfers between devices, extended_2(): before = lax.ppermute(last, axis, up)  14.2 us
    dynamic_update_slice x4, local copies, waits for them, and re-layouts, one_position(): lax.dynamic_update_slice(frame_sum, previous + addition, (zero_index, row...  13.6 us
    sub x4, other arithmetic, one_position(): grad_im = grad_im + patch_re[None] * change_im - patch_im[None] * change_re  9.93 us
  transfers between devices with their start and end apart: 10, of which 4 were waited for; matrix products, arithmetic and copies ran while one was open for 5% of the time, Pallas kernels for 0%

profile of v1, /device:TPU:0, one launch (start us, length us, event | category | flops | bytes accessed | tf_op | source)
XLA Modules:
  0.0 387.0 jit_solution(14822037529138080412)
XLA Ops:
  8.7 3.1 collective-permute-start
  15.1 5.1 %collective-permute-start.2 = (f32[2,384,128]{2,1,0:T(8,128)S(1)}, f32[2,384,128]{2,1,0:T(8,128)S(1)}, u32[]{:S(2)}, u32[]{:S(2)}) collective-permute-start(f32[2,384,128]{2,1,0:T(8,128)S(1)} %get-tuple-element.613), channel_id=1, source_target_pairs={{0,1},{2,3},{4,5},{6,7},{8,9},{10,11},{12,13},{14,15},{16,17},{18,... | collective-permute-start | bytes 1179656 | tf_op jit(solution)/shard_map/ppermute | solution.py:22
  21.7 5.7 %collective-permute-done.2 = f32[2,384,128]{2,1,0:T(8,128)S(1)} collective-permute-done((f32[2,384,128]{2,1,0:T(8,128)S(1)}, f32[2,384,128]{2,1,0:T(8,128)S(1)}, u32[]{:S(2)}, u32[]{:S(2)}) %collective-permute-start.2) | collective-permute-done | bytes 393248 | tf_op jit(solution)/shard_map/ppermute | solution.py:22
  27.3 4.7 %collective-permute-done.3 = f32[2,384,128]{2,1,0:T(8,128)S(1)} collective-permute-done((f32[2,384,128]{2,1,0:T(8,128)S(1)}, f32[2,384,128]{2,1,0:T(8,128)S(1)}, u32[]{:S(2)}, u32[]{:S(2)}) %collective-permute-start.3) | collective-permute-done | bytes 393248 | tf_op jit(solution)/shard_map/ppermute | solution.py:23
  35.1 116.9 %while.34 = (s32[]{:T(128)}, f32[12,128,128]{2,1,0:T(8,128)}, f32[12,128,128]{2,1,0:T(8,128)}, f32[128,128]{1,0:T(8,128)}, f32[3,384,512]{2,1,0:T(8,128)}, /*ind...) while((s32[]{:T(128)}, f32[12,128,128]{2,1,0:T(8,128)}, ...), condition=%wide.region_6.7_spmd.clone, body=%wide.region_1.6_spmd.clone.sunk | while | flops 4844257280 | bytes 53870996 | solution.py:200
  43.3 2.7 fusion.162
  46.2 2.8 convolution_bitcast_fusion.4
  49.4 2.8 fusion.164
  52.4 2.7 convolution_bitcast_fusion.5
  59.7 2.8 dynamic_update_slice.12
  73.7 2.8 convolution_bitcast_fusion.4
  76.9 2.8 fusion.164
  79.9 2.7 convolution_bitcast_fusion.5
  84.7 2.8 fusion.166
  88.7 2.8 dynamic_update_slice.12
  102.8 2.8 convolution_bitcast_fusion.4
  106.0 2.8 fusion.164
  108.9 2.7 convolution_bitcast_fusion.5
  113.8 2.8 fusion.166
  117.8 4.0 %dynamic_update_slice.12 = f32[3,384,512]{2,1,0:T(8,128)} dynamic-update-slice(f32[3,384,512]{2,1,0:T(8,128)} %get-tuple-element.772, f32[3,128,128]{2,1,0:T(8,128)S(1)} %maximum_add_fusion.2, s32[]{:T(128)} %constant.327.clone.1..sunk, s32[]{:T(128)S(6)} %select_n.67, s32[]{:T(128)S(6)} %select_n.68) | dynamic-update-slice | bytes 393220 | tf_op jit(solution)/shard_map/while/body/eval_jaxpr/dynamic_update_slice | solution.py:184
  130.1 2.7 fusion.162
  133.0 2.8 convolution_bitcast_fusion.4
  136.2 2.8 fusion.164
  139.2 2.7 convolution_bitcast_fusion.5
  144.0 2.8 fusion.166
  148.0 4.0 %dynamic_update_slice.12 = f32[3,384,512]{2,1,0:T(8,128)} dynamic-update-slice(f32[3,384,512]{2,1,0:T(8,128)} %get-tuple-element.772, f32[3,128,128]{2,1,0:T(8,128)S(1)} %maximum_add_fusion.2, s32[]{:T(128)} %constant.327.clone.1..sunk, s32[]{:T(128)S(6)} %select_n.67, s32[]{:T(128)S(6)} %select_n.68) | dynamic-update-slice | bytes 393220 | tf_op jit(solution)/shard_map/while/body/eval_jaxpr/dynamic_update_slice | solution.py:184
  152.0 2.9 fusion.66
  154.9 3.7 collective-permute-start.4
  173.7 73.1 %all-reduce = (f32[]{:T(128)}, f32[]{:T(128)}) all-reduce(f32[]{:T(128)} %reduce_sum.93, f32[]{:T(128)} %get-tuple-element.473), channel_id=1, replica_groups=mesh['scan'=16,'tile'=2] {'scan','tile'}, use_global_device_ids=true, to_apply=%region_13.14 | all-reduce | flops 2 | bytes 16 | tf_op jit(solution)/shard_map/psum | solution.py:102
  256.2 89.1 %all-reduce.6.cloned.1.call-done = (f32[24,16384]{1,0:T(8,128)}, f32[1,16384]{1,0:T(1,128)}) async-done(((f32[24,16384]{1,0:T(8,128)}, f32[1,16384]{1,0:T(1,128)}), (f32[24,16384]{1,0:T(8,128)}, f32[1,16384]{1,0:T(1,128)})) %all-reduce.6.cloned.1.call-update) | async-done | bytes 1638416 | tf_op jit(solution)/shard_map/psum | solution.py:213
  349.7 4.6 %slice.446 = f32[12,16384]{1,0:T(8,128)S(1)} slice(f32[24,16384]{1,0:T(8,128)S(1)} %bitcast_add_fusion), slice={[1:24:2], [0:16384:1]} | slice | bytes 1572864 | tf_op jit(solution)/shard_map/slice | solution.py:76
  354.3 5.7 %slice.445 = f32[12,16384]{1,0:T(8,128)S(1)} slice(f32[24,16384]{1,0:T(8,128)} %copy-done.5), slice={[0:24:2], [0:16384:1]} | slice | bytes 1572864 | tf_op jit(solution)/shard_map/slice | solution.py:75
  (177 shorter events, 92.7 us)
Async XLA Ops:
  7.2 7.8 %copy-start.8 = (f32[2,128,256]{2,1,0:T(8,128)S(1)}, f32[2,128,256]{2,1,0:T(8,128)}, u32[]{:S(2)}) copy-start(f32[2,128,256]{2,1,0:T(8,128)} %param.28) | copy-start | bytes 786436
  7.2 242.0 %all-reduce.8.cloned.1.call-start = ((), (), s32[]{:S(2)}) async-start(), calls=%async_computation.1 | async-start | bytes 3276800 | tf_op jit(solution)/shard_map/psum | solution.py:214
  7.2 7.8 %collective-permute-start.1 = (f32[2,128,256]{2,1,0:T(8,128)}, f32[2,128,256]{2,1,0:T(8,128)S(1)}, u32[]{:S(2)}, u32[]{:S(2)}) collective-permute-start(f32[2,128,256]{2,1,0:T(8,128)} %param.28), channel_id=1, source_target_pairs={{2,0},{4,2},{6,4},{8,6},{10,8},{12,10},{14,12},{16,14},{18,16},{20... | collective-permute-start | bytes 786440 | tf_op jit(solution)/shard_map/ppermute | solution.py:23
  8.7 6.3 %collective-permute-start = (f32[2,128,256]{2,1,0:T(8,128)}, f32[2,128,256]{2,1,0:T(8,128)S(1)}, u32[]{:S(2)}, u32[]{:S(2)}) collective-permute-start(f32[2,128,256]{2,1,0:T(8,128)} %param.28), channel_id=1, source_target_pairs={{0,2},{2,4},{4,6},{6,8},{8,10},{10,12},{12,14},{14,16},{16,18},{18... | collective-permute-start | bytes 786440 | tf_op jit(solution)/shard_map/ppermute | solution.py:22
  15.0 6.5 %copy-start.3 = (f32[12,2,128,128]{3,2,1,0:T(8,128)S(1)}, f32[12,2,128,128]{3,2,1,0:T(8,128)}, u32[]{:S(2)}) copy-start(f32[12,2,128,128]{3,2,1,0:T(8,128)} %param.26) | copy-start | bytes 4718596
  15.1 12.2 %collective-permute-start.2 = (f32[2,384,128]{2,1,0:T(8,128)S(1)}, f32[2,384,128]{2,1,0:T(8,128)S(1)}, u32[]{:S(2)}, u32[]{:S(2)}) collective-permute-start(f32[2,384,128]{2,1,0:T(8,128)S(1)} %get-tuple-element.613), channel_id=1, source_target_pairs={{0,1},{2,3},{4,5},{6,7},{8,9},{10,11},{12,13},{14,15},{16,17},{18,... | collective-permute-start | bytes 1179656 | tf_op jit(solution)/shard_map/ppermute | solution.py:22
  20.2 11.9 %collective-permute-start.3 = (f32[2,384,128]{2,1,0:T(8,128)S(1)}, f32[2,384,128]{2,1,0:T(8,128)S(1)}, u32[]{:S(2)}, u32[]{:S(2)}) collective-permute-start(f32[2,384,128]{2,1,0:T(8,128)S(1)} %get-tuple-element.614), channel_id=1, source_target_pairs={{1,0},{3,2},{5,4},{7,6},{9,8},{11,10},{13,12},{15,14},{17,16},{19,... | collective-permute-start | bytes 1179656 | tf_op jit(solution)/shard_map/ppermute | solution.py:23
  57.2 1.5 copy-start.6
  57.2 1.5 copy-start.7
  84.7 2.9 copy-start.6
  84.7 2.8 copy-start.7
  113.7 2.9 copy-start.6
  113.8 2.8 copy-start.7
  144.0 2.9 copy-start.6
  144.0 2.8 copy-start.7
  152.0 7.9 %copy-start = (f32[12,128,128]{2,1,0:T(8,128)S(1)}, f32[12,128,128]{2,1,0:T(8,128)}, u32[]{:S(2)}) copy-start(f32[12,128,128]{2,1,0:T(8,128)} %get-tuple-element.471) | copy-start | bytes 2359300
  152.0 7.9 %copy-start.1 = (f32[12,128,128]{2,1,0:T(8,128)S(1)}, f32[12,128,128]{2,1,0:T(8,128)}, u32[]{:S(2)}) copy-start(f32[12,128,128]{2,1,0:T(8,128)} %get-tuple-element.470) | copy-start | bytes 2359300
  154.9 7.5 %collective-permute-start.4 = (f32[3,128,512]{2,1,0:T(8,128)}, f32[3,128,512]{2,1,0:T(8,128)S(1)}, u32[]{:S(2)}, u32[]{:S(2)}) collective-permute-start(f32[3,128,512]{2,1,0:T(8,128)} %get-tuple-element.609), channel_id=1, source_target_pairs={{0,2},{2,4},{4,6},{6,8},{8,10},{10,12},{12,14},{14,16},{16,18},{18... | collective-permute-start | bytes 2359304 | tf_op jit(solution)/shard_map/ppermute | solution.py:22
  158.5 7.1 %collective-permute-start.5 = (f32[3,128,512]{2,1,0:T(8,128)}, f32[3,128,512]{2,1,0:T(8,128)}, u32[]{:S(2)}, u32[]{:S(2)}) collective-permute-start(f32[3,128,512]{2,1,0:T(8,128)} %get-tuple-element.610), channel_id=1, source_target_pairs={{2,0},{4,2},{6,4},{8,6},{10,8},{12,10},{14,12},{16,14},{18,16},{20... | collective-permute-start | bytes 2359304 | tf_op jit(solution)/shard_map/ppermute | solution.py:23
  162.2 1.7 copy-start.2
  162.3 183.0 %all-reduce.6.cloned.1.call-start = ((), (), s32[]{:S(2)}) async-start(), calls=%async_computation | async-start | bytes 3276800 | tf_op jit(solution)/shard_map/psum | solution.py:213
  168.3 81.0 %collective-permute-start.6 = (f32[3,640,128]{2,1,0:T(8,128)}, f32[3,640,128]{2,1,0:T(8,128)}, u32[]{:S(2)}, u32[]{:S(2)}) collective-permute-start(f32[3,640,128]{2,1,0:T(8,128)} %get-tuple-element.608), channel_id=1, source_target_pairs={{0,1},{2,3},{4,5},{6,7},{8,9},{10,11},{12,13},{14,15},{16,17},{18,... | collective-permute-start | bytes 2949128 | tf_op jit(solution)/shard_map/ppermute | solution.py:22
  170.7 79.6 %collective-permute-start.7 = (f32[3,640,128]{2,1,0:T(8,128)}, f32[3,640,128]{2,1,0:T(8,128)}, u32[]{:S(2)}, u32[]{:S(2)}) collective-permute-start(f32[3,640,128]{2,1,0:T(8,128)} %get-tuple-element.607), channel_id=1, source_target_pairs={{1,0},{3,2},{5,4},{7,6},{9,8},{11,10},{13,12},{15,14},{17,16},{19,... | collective-permute-start | bytes 2949128 | tf_op jit(solution)/shard_map/ppermute | solution.py:23
  250.2 5.2 %copy-start.9 = (f32[2,128,256]{2,1,0:T(8,128)S(1)}, f32[2,128,256]{2,1,0:T(8,128)}, u32[]{:S(2)}) copy-start(f32[2,128,256]{2,1,0:T(8,128)} %param.28) | copy-start | bytes 786436
  252.3 93.9 %copy-start.4 = (f32[12,2,128,128]{3,2,1,0:T(8,128)S(1)}, f32[12,2,128,128]{3,2,1,0:T(8,128)}, u32[]{:S(2)}) copy-start(f32[12,2,128,128]{3,2,1,0:T(8,128)} %param.26) | copy-start | bytes 4718596
  348.6 1.1 copy-start.5
Sparse Core Ops, SparseCore 0:
  162.4 70.1 all-reduce.7
  249.4 95.8 all-reduce.5
